TPU v7x, 32 devices: a whole 2x2x4 slice. The times are simulated.
32 devices in a mesh: dp: 2 (over x), row: 4 (over y, core), col: 4 (over z).
Axes of the slice: x: 2, y: 2, z: 4, core: 2. Of those that a mesh axis runs over, the one named last changes fastest.
Arguments:
- latents: float32 [24, 32, 128], P(('dp', 'row')), may hold values from -6 to 6
- labels: int32 [24], P(('dp', 'row')), may hold values from 0 to 999
- step_index: int32 [24], P(('dp', 'row')), may hold values from 1 to 8
- seeds: int32 [24], P(('dp', 'row')), may hold values from 0 to 2147483646
- class_table: bfloat16 [1000, 1152], replicated, may hold values from -6 to 6
- teacher_patch: bfloat16 [16, 1152], replicated, may hold values from -1.5 to 1.5
- teacher_mod: bfloat16 [1152, 3, 1152], P(('dp', 'row'), None, 'col'), may hold values from -0.1875 to 0.1875
- teacher_up: bfloat16 [1152, 4608], P(('dp', 'row'), 'col'), may hold values from -0.1875 to 0.1875
- teacher_down: bfloat16 [1152, 4608], P(('dp', 'row'), 'col'), may hold values from -0.09375 to 0.09375
- teacher_out: bfloat16 [16, 1152], replicated, may hold values from -0.1875 to 0.1875
- student_patch: bfloat16 [16, 1152], replicated, may hold values from -1.5 to 1.5
- student_mod: bfloat16 [1152, 3, 1152], P(('dp', 'row'), None, 'col'), may hold values from -0.1875 to 0.1875
- student_up: bfloat16 [1152, 4608], P(('dp', 'row'), 'col'), may hold values from -0.1875 to 0.1875
- student_down: bfloat16 [1152, 4608], P(('dp', 'row'), 'col'), may hold values from -0.09375 to 0.09375
- student_out: bfloat16 [16, 1152], replicated, may hold values from -0.1875 to 0.1875
Outputs:
- up_gradient: float32 [1152, 4608], P(('dp', 'row'), 'col')
- down_gradient: float32 [1152, 4608], P(('dp', 'row'), 'col')
All inputs are finite; a program needn't handle non-finite values.
Results may differ from a plain program's by a relative error of at most 0.002.
Values may be sent and summed in bfloat16 or wider, within the bound.
No kernel may reach another device: no remote copies, remote signals or barrier semaphores. Data moves between devices by JAX's collectives and lax.ppermute only.
A program may use at most 128 MiB of HBM per device.

v0:
```python
import math
import jax
import jax.numpy as jnp
from jax import lax
from jax.sharding import PartitionSpec as P

D = 1152
CLASSES = 1000
SEQ = 256
PATCH = 16
STEPS = 8
HALF_PI = 0.5 * math.pi
ROOT_TWO_PI = math.sqrt(2.0 / math.pi)


def plan(times):
    return (jnp.cos(HALF_PI * times), jnp.sin(HALF_PI * times))


def mixing(value):
    amount = jnp.int32(16)
    value = value ^ lax.shift_right_logical(value, amount)
    value = value * 73244475
    value = value ^ lax.shift_right_logical(value, amount)
    value = value * 73244475
    value = value ^ lax.shift_right_logical(value, amount)
    return value


def noise_of(seeds):
    total = SEQ * PATCH
    places = jnp.arange(total, dtype=jnp.int32).reshape(1, total // 128, 128)
    mixed = mixing(seeds[:, None, None] * 1103515245 + places * 40503 + 12345)
    uniform = (lax.shift_right_logical(mixed, jnp.int32(8)).astype(jnp.float32) + 0.5) * (
        1.0 / 16777216.0
    )
    return math.sqrt(2.0) * lax.erf_inv(2.0 * uniform - 1.0)


def time_features(times):
    half = D // 2
    freqs = jnp.exp(-math.log(10000.0) * jnp.arange(half, dtype=jnp.float32) / half)
    angle = (1000.0 * times)[:, None] * freqs[None, :]
    return jnp.concatenate([jnp.cos(angle), jnp.sin(angle)], axis=1)


def condition(times, labels, class_table):
    onehot = (labels[:, None] == jnp.arange(CLASSES, dtype=jnp.int32)[None, :]).astype(jnp.bfloat16)
    embedded = jnp.dot(onehot, class_table, preferred_element_type=jnp.float32)
    return jax.nn.silu(embedded + time_features(times)).astype(jnp.bfloat16)


def positions():
    quarter = D // 4
    omega = 1.0 / 10000.0 ** (jnp.arange(quarter, dtype=jnp.float32) / quarter)
    side = math.isqrt(SEQ)
    cells = jnp.arange(SEQ, dtype=jnp.int32)
    grid_row = (cells // side).astype(jnp.float32)
    grid_col = (cells % side).astype(jnp.float32)
    row_angle = grid_row[:, None] * omega[None, :]
    col_angle = grid_col[:, None] * omega[None, :]
    return jnp.concatenate(
        [jnp.sin(row_angle), jnp.cos(row_angle), jnp.sin(col_angle), jnp.cos(col_angle)], axis=1
    )


def layer_norm(values):
    center = values - jnp.mean(values, axis=-1, keepdims=True)
    spread = jnp.mean(center * center, axis=-1, keepdims=True)
    reciprocal = lax.rsqrt(spread + 1e-06)
    return (center * reciprocal, reciprocal)


def gelu_slope(pre):
    inner = ROOT_TWO_PI * (pre + 0.044715 * pre * pre * pre)
    tangent = jnp.tanh(inner)
    return 0.5 * (1.0 + tangent) + 0.5 * pre * (1.0 - tangent * tangent) * ROOT_TWO_PI * (
        1.0 + 3.0 * 0.044715 * pre * pre
    )


def contract_last(left, right):
    return lax.dot_general(
        left, right, (((1,), (1,)), ((), ())), preferred_element_type=jnp.float32
    )


def contract_first(left, right):
    return lax.dot_general(
        left, right, (((0,), (0,)), ((), ())), preferred_element_type=jnp.float32
    )


def network(state, mods, patch_weight, out_weight, pos, up_product, down_product):
    samples = state.shape[0]
    tokens = state.reshape(samples * SEQ, PATCH).astype(jnp.bfloat16)
    base = (
        jnp.dot(tokens, patch_weight, preferred_element_type=jnp.float32).reshape(samples, SEQ, D)
        + pos[None]
    )
    shift = mods[:, 0][:, None, :]
    scale = mods[:, 1][:, None, :]
    gate = mods[:, 2][:, None, :]
    normed, _ = layer_norm(base)
    act = (normed * (1.0 + scale) + shift).astype(jnp.bfloat16).reshape(samples * SEQ, D)
    pre = up_product(act)
    hidden = jax.nn.gelu(pre, approximate=True).astype(jnp.bfloat16)
    partial_out = down_product(hidden).astype(jnp.bfloat16)
    mixed = lax.psum(partial_out, "col").astype(jnp.float32)
    later = base + gate * mixed.reshape(samples, SEQ, D)
    final, reciprocal = layer_norm(later)
    velocity = contract_last(final.astype(jnp.bfloat16).reshape(samples * SEQ, D), out_weight)
    return (
        velocity.reshape(samples, SEQ * PATCH // 128, 128),
        (act, pre, hidden, final, reciprocal, gate, out_weight),
    )


def reduce_gradient(left, right):
    return lax.psum_scatter(
        contract_first(left, right), ("dp", "row"), scatter_dimension=0, tiled=True
    )


def body(
    latents,
    labels,
    step_index,
    seeds,
    class_table,
    teacher_patch,
    teacher_mod,
    teacher_up,
    teacher_down,
    teacher_out,
    student_patch,
    student_mod,
    student_up,
    student_down,
    student_out,
):
    samples = latents.shape[0]
    batch_total = samples * lax.axis_size(("dp", "row"))
    pos = positions()
    all_labels, all_steps = (
        lax.all_gather(labels, ("dp", "row"), axis=0, tiled=True),
        lax.all_gather(step_index, ("dp", "row"), axis=0, tiled=True),
    )
    all_now = all_steps.astype(jnp.float32) / STEPS
    cond_now = condition(all_now, all_labels, class_table)
    cond_mid = condition(all_now - 0.5 / STEPS, all_labels, class_table)
    own_rows = teacher_mod.shape[0]
    offset = lax.axis_index(("dp", "row")) * own_rows
    rows_now = lax.dynamic_slice_in_dim(cond_now, offset, own_rows, 1)
    rows_mid = lax.dynamic_slice_in_dim(cond_mid, offset, own_rows, 1)
    teacher_part = jnp.einsum(
        "nkd,dcf->nkcf",
        jnp.stack([rows_now, rows_mid], axis=1),
        teacher_mod,
        preferred_element_type=jnp.float32,
    )
    student_part = jnp.einsum(
        "nd,dcf->ncf", rows_now, student_mod, preferred_element_type=jnp.float32
    )[:, None]
    teacher_sums, student_sums = (
        lax.psum_scatter(teacher_part, ("dp", "row"), scatter_dimension=0, tiled=True),
        lax.psum_scatter(student_part, ("dp", "row"), scatter_dimension=0, tiled=True),
    )
    teacher_mods, student_mods = (
        lax.all_gather(teacher_sums, "col", axis=3, tiled=True),
        lax.all_gather(student_sums, "col", axis=3, tiled=True),
    )
    now = step_index.astype(jnp.float32) / STEPS
    alpha, sigma = plan(now[:, None, None])
    alpha_mid, sigma_mid = plan((now - 0.5 / STEPS)[:, None, None])
    alpha_end, sigma_end = plan((now - 1.0 / STEPS)[:, None, None])
    noisy = alpha * latents + sigma * noise_of(seeds)
    up_panel, down_panel = (
        lax.all_gather(teacher_up, ("dp", "row"), axis=0, tiled=True),
        lax.all_gather(teacher_down, ("dp", "row"), axis=0, tiled=True),
    )

    def teacher_up_product(act):
        return jnp.dot(act, up_panel, preferred_element_type=jnp.float32)

    def teacher_down_product(hidden):
        return contract_last(hidden, down_panel)

    first_v, _ = network(
        noisy,
        teacher_mods[:, 0],
        teacher_patch,
        teacher_out,
        pos,
        teacher_up_product,
        teacher_down_product,
    )
    first_x = alpha * noisy - sigma * first_v
    halfway = alpha_mid * first_x + sigma_mid * (noisy - alpha * first_x) / sigma
    second_v, _ = network(
        halfway,
        teacher_mods[:, 1],
        teacher_patch,
        teacher_out,
        pos,
        teacher_up_product,
        teacher_down_product,
    )
    second_x = alpha_mid * halfway - sigma_mid * second_v
    landing = alpha_end * second_x + sigma_end * (halfway - alpha_mid * second_x) / sigma_mid
    ratio = sigma_end / sigma
    target = (landing - ratio * noisy) / (alpha_end - ratio * alpha)

    def student_up_product(act):
        return jnp.dot(
            act,
            lax.all_gather(student_up, ("dp", "row"), axis=0, tiled=True),
            preferred_element_type=jnp.float32,
        )

    student_panel = lax.all_gather(student_down, ("dp", "row"), axis=0, tiled=True)

    def student_down_product(hidden):
        return contract_last(hidden, student_panel)

    student_v, saved = network(
        noisy,
        student_mods[:, 0],
        student_patch,
        student_out,
        pos,
        student_up_product,
        student_down_product,
    )
    student_x = alpha * noisy - sigma * student_v
    weight = jnp.maximum(alpha * alpha / (sigma * sigma), 1.0)
    back_velocity = (-2.0 * sigma * weight * (student_x - target) / batch_total).reshape(
        samples * SEQ, PATCH
    )
    act, pre, hidden, final, reciprocal, gate_share, out_share = saved
    back_final = jnp.dot(
        back_velocity, out_share.astype(jnp.float32), precision=lax.Precision.HIGHEST
    ).reshape(samples, SEQ, -1)
    centre = jnp.mean(back_final, axis=2, keepdims=True)
    along = jnp.mean(back_final * final, axis=2, keepdims=True)
    back_mixed = (
        (gate_share * (reciprocal * (back_final - centre - final * along)))
        .astype(jnp.bfloat16)
        .reshape(samples * SEQ, D)
    )
    down_gradient = reduce_gradient(back_mixed, hidden)
    back_hidden = jnp.dot(back_mixed, student_panel, preferred_element_type=jnp.float32)
    back_pre = (back_hidden * gelu_slope(pre)).astype(jnp.bfloat16)
    up_gradient = reduce_gradient(act, back_pre)
    return (up_gradient, down_gradient)


def solution(mesh):
    placed = (
        P(("dp", "row"), None, None),
        P(("dp", "row")),
        P(("dp", "row")),
        P(("dp", "row")),
        P(),
        P(),
        P(("dp", "row"), None, "col"),
        P(("dp", "row"), "col"),
        P(("dp", "row"), "col"),
        P(),
        P(),
        P(("dp", "row"), None, "col"),
        P(("dp", "row"), "col"),
        P(("dp", "row"), "col"),
        P(),
    )
    return jax.shard_map(
        body,
        mesh=mesh,
        in_specs=placed,
        out_specs=(P(("dp", "row"), "col"), P(("dp", "row"), "col")),
        check_vma=False,
    )
```

profile of v0, /device:TPU:0, one launch (start us, length us, event | category | flops | bytes accessed | tf_op | source)
XLA Modules:
  0.0 598.2 jit_solution(1822111172915230698)
XLA Ops:
  11.2 9.5 %all-reduce.4 = (s32[24]{0:T(128)S(1)}, s32[24]{0:T(128)S(1)}) all-reduce(s32[24]{0:T(128)S(1)} %dynamic-update-slice, s32[24]{0:T(128)S(1)} %dynamic-update-slice.1), channel_id=1, replica_groups=mesh['dp'=2,'row'=4,'col'=4] {'dp','row'}, use_global_device_ids=true, to_apply=%add | all-reduce | flops 48 | bytes 384
  30.0 2.8 multiply_cosine_fusion
  40.5 2.5 multiply_reduce_fusion.6
  44.3 33.5 %all-reduce.13.cloned.1.call-done = (f32[24,1,3,288]{3,1,2,0:T(1,128)}, f32[24,2,3,288]{3,1,2,0:T(2,128)}) async-done(((f32[24,1,3,288]{3,1,2,0:T(1,128)}, f32[24,2,3,288]{3,1,2,0:T(2,128)}), (f32[24,1,3,288]{3,1,2,0:T(1,128)}, f32[24,2,3,288]{3,1,2,0:T(2,128)})) %all-reduce.13.cloned.1.call-update) | async-done | bytes 248848
  81.2 62.1 %all_gather.29 = f32[3,2,3,1152]{2,1,0,3:T(2,128)S(1)} all-gather(f32[3,2,3,288]{2,1,0,3:T(2,128)} %copy.57), channel_id=1, replica_groups=mesh['dp'=2,'row'=4,'col'=4] {'col'}, dimensions={3}, use_global_device_ids=true | all-gather | bytes 103680 | tf_op jit(solution)/shard_map/all_gather | solution.py:170
  143.3 3.9 fusion.94
  147.1 4.6 copy.81
  151.7 4.6 copy.82
  158.0 38.8 %all_gather.26 = f32[3,1,3,1152]{2,1,0,3:T(1,128)} all-gather(f32[3,1,3,288]{2,1,0,3:T(1,128)} %copy.52), channel_id=1, replica_groups=mesh['dp'=2,'row'=4,'col'=4] {'col'}, dimensions={3}, use_global_device_ids=true | all-gather | bytes 51840 | tf_op jit(solution)/shard_map/all_gather | solution.py:171
  196.9 4.6 copy.53
  204.0 3.1 add_convert_fusion.1
  207.2 4.5 add_convert_fusion.2
  211.7 9.5 %convolution_convert_fusion.1 = bf16[768,1152]{1,0:T(8,128)(2,1)} fusion(bf16[1152,1152]{1,0:T(8,128)(2,1)} %all-gather.11.cloned.1.call-done, bf16[768,1152]{1,0:T(8,128)(2,1)} %bitcast.116, bf16[1152,1152]{1,0:T(8,128)(2,1)} %all-gather.9.cloned.1.call-done), kind=kOutput, calls=%fused_computation.56 | convolution fusion | flops 4085710848 | bytes 8847360 | tf_op jit(solution)/shard_map/dot_general | solution.py:83
  225.0 6.7 %fusion.106 = f32[768,1152]{1,0:T(8,128)} fusion(bf16[768,1152]{1,0:T(8,128)(2,1)} %bitcast.109, bf16[1152,1152]{1,0:T(8,128)(2,1)} %all-gather.5.cloned.1.call-done), kind=kOutput, calls=%fused_computation.198 | convolution fusion | flops 2038431744 | bytes 7962624 | tf_op jit(solution)/shard_map/dot_general | solution.py:215
  231.7 7.3 %convolution_convert_fusion.2 = bf16[768,1152]{1,0:T(8,128)(2,1)} fusion(bf16[1152,1152]{1,0:T(8,128)(2,1)} %all-gather.7.cloned.1.call-done, f32[768,1152]{1,0:T(8,128)} %fusion.106), kind=kOutput, calls=%fused_computation.57 | convolution fusion | flops 2047279104 | bytes 7962624 | tf_op jit(solution)/shard_map/dot_general | solution.py:83
  238.9 54.8 %all-reduce.11.cloned.1.call-done = bf16[3,256,1152]{2,1,0:T(8,128)(2,1)} async-done(((bf16[3,256,1152]{2,1,0:T(8,128)(2,1)}), bf16[3,256,1152]{2,1,0:T(8,128)(2,1)}) %all-reduce.11.cloned.1.call-update) | async-done | bytes 1769488 | tf_op jit(solution)/shard_map/psum | solution.py:109
  305.2 9.7 %convolution_convert_fusion = bf16[768,1152]{1,0:T(8,128)(2,1)} fusion(bf16[1152,1152]{1,0:T(8,128)(2,1)} %all-gather.11.cloned.1.call-done, bf16[768,1152]{1,0:T(8,128)(2,1)} %bitcast.117, bf16[1152,1152]{1,0:T(8,128)(2,1)} %all-gather.9.cloned.1.call-done), kind=kOutput, calls=%fused_computation.55 | convolution fusion | flops 4085710848 | bytes 8847360 | tf_op jit(solution)/shard_map/dot_general | solution.py:83
  316.9 131.0 %all-reduce.15.cloned.1.call-done = (bf16[3,256,1152]{2,1,0:T(8,128)(2,1)}, bf16[3,256,1152]{2,1,0:T(8,128)(2,1)}) async-done(((bf16[3,256,1152]{2,1,0:T(8,128)(2,1)}, bf16[3,256,1152]{2,1,0:T(8,128)(2,1)}), (bf16[3,256,1152]{2,1,0:T(8,128)(2,1)}, bf16[3,256,1152]{2,1,0:T(8,128)(2,1)})) %all-reduce.15.cloned.1.call-update) | async-done | bytes 3538960 | tf_op jit(solution)/shard_map/psum | solution.py:109
  447.9 3.1 fusion.92
  462.0 4.6 fusion.90
  469.2 5.0 fusion.87
  474.6 12.3 %fusion.110 = f32[1152,1152]{1,0:T(8,128)} fusion(bf16[768,1152]{1,0:T(8,128)(2,1)} %bitcast.110, f32[768,1152]{1,0:T(8,128)} %fusion.106, bf16[768,1152]{1,0:T(8,128)(2,1)} %bitcast.115, bf16[1152,1152]{1,0:T(8,128)(2,1)} %all-gather.7.cloned.1.call-done), kind=kOutput, calls=%fused_computation.202 | convolution fusion | flops 4093673472 | bytes 15040512 | tf_op jit(solution)/shard_map/dot_general | solution.py:89
  486.9 43.4 %reduce-scatter.5.cloned.1.call-done = f32[144,1152]{1,0:T(8,128)} async-done(((f32[1152,1152]{1,0:T(8,128)}), f32[144,1152]{1,0:T(8,128)}) %reduce-scatter.5.cloned.1.call-update) | async-done | bytes 663568 | tf_op jit(solution)/shard_map/reduce_scatter | solution.py:120
  530.3 60.9 %reduce-scatter.3.cloned.1.call-done = f32[144,1152]{1,0:T(8,128)} async-done(((f32[1152,1152]{1,0:T(8,128)}), f32[144,1152]{1,0:T(8,128)}) %reduce-scatter.3.cloned.1.call-update) | async-done | bytes 663568 | tf_op jit(solution)/shard_map/reduce_scatter | solution.py:120
  (159 shorter events, 59.2 us)
Async XLA Ops:
  7.2 14.0 %copy-start = (bf16[1000,1152]{1,0:T(8,128)(2,1)S(1)}, bf16[1000,1152]{1,0:T(8,128)(2,1)}, u32[]{:S(2)}) copy-start(bf16[1000,1152]{1,0:T(8,128)(2,1)} %param.19) | copy-start | bytes 6912004
  7.2 20.4 %copy-start.28 = (s32[3]{0:T(128)S(1)}, s32[3]{0:T(128)}, u32[]{:S(2)}) copy-start(s32[3]{0:T(128)} %param.17) | copy-start | bytes 40
  7.2 16.6 %copy-start.10 = (bf16[144,3,288]{2,0,1:T(8,128)(2,1)S(1)}, bf16[144,3,288]{2,0,1:T(8,128)(2,1)}, u32[]{:S(2)}) copy-start(bf16[144,3,288]{2,0,1:T(8,128)(2,1)} %param.26) | copy-start | bytes 746500
  7.2 21.1 %copy-start.29 = (s32[3]{0:T(128)S(1)}, s32[3]{0:T(128)}, u32[]{:S(2)}) copy-start(s32[3]{0:T(128)} %param.18) | copy-start | bytes 40
  7.2 21.1 %copy-start.19 = (f32[3,32,128]{2,1,0:T(8,128)S(1)}, f32[3,32,128]{2,1,0:T(8,128)}, u32[]{:S(2)}) copy-start(f32[3,32,128]{2,1,0:T(8,128)} %param.15) | copy-start | bytes 147460
  7.2 70.6 %all-reduce.13.cloned.1.call-start = ((), (), s32[]{:S(2)}) async-start(), calls=%async_computation.9 | async-start | bytes 663552
  24.9 186.8 %all-gather.11.cloned.1.call-start = ((), (), s32[]{:S(2)}) async-start(), calls=%async_computation.5 | async-start | bytes 2985984 | tf_op jit(solution)/shard_map/all_gather | solution.py:180
  25.6 186.1 %all-gather.9.cloned.1.call-start = ((), (), s32[]{:S(2)}) async-start(), calls=%async_computation.4 | async-start | bytes 2985984 | tf_op jit(solution)/shard_map/all_gather | solution.py:179
  26.4 198.6 %all-gather.5.cloned.1.call-start = ((), (), s32[]{:S(2)}) async-start(), calls=%async_computation.2 | async-start | bytes 2985984 | tf_op jit(solution)/shard_map/all_gather | solution.py:217
  27.0 204.7 %all-gather.7.cloned.1.call-start = ((), (), s32[]{:S(2)}) async-start(), calls=%async_computation.3 | async-start | bytes 2985984 | tf_op jit(solution)/shard_map/all_gather | solution.py:221
  27.5 266.3 %all-reduce.11.cloned.1.call-start = ((), (), s32[]{:S(2)}) async-start(), calls=%async_computation.6 | async-start | bytes 3538944 | tf_op jit(solution)/shard_map/psum | solution.py:109
  34.2 3.3 copy-start.4
  34.2 3.3 copy-start.7
  34.2 3.3 copy-start.20
  36.4 3.5 copy-start.21
  201.4 5.7 copy-start.23
  201.4 5.7 copy-start.24
  221.2 226.7 %all-reduce.15.cloned.1.call-start = ((), (), s32[]{:S(2)}) async-start(), calls=%async_computation.10 | async-start | bytes 7077888 | tf_op jit(solution)/shard_map/psum | solution.py:109
  300.1 2.6 copy-start.18
  314.9 215.4 %reduce-scatter.5.cloned.1.call-start = ((), (), s32[]{:S(2)}) async-start(), calls=%async_computation.8 | async-start | bytes 5971968 | tf_op jit(solution)/shard_map/reduce_scatter | solution.py:120
  462.0 4.7 copy-start.3
  462.0 4.7 copy-start.13
  474.3 116.9 %reduce-scatter.3.cloned.1.call-start = ((), (), s32[]{:S(2)}) async-start(), calls=%async_computation.7 | async-start | bytes 5971968 | tf_op jit(solution)/shard_map/reduce_scatter | solution.py:120
  474.6 116.6 %copy-start.1 = (bf16[1000,1152]{1,0:T(8,128)(2,1)S(1)}, bf16[1000,1152]{1,0:T(8,128)(2,1)}, u32[]{:S(2)}) copy-start(bf16[1000,1152]{1,0:T(8,128)(2,1)} %param.19) | copy-start | bytes 6912004
  (16 other events, 26.4 us)
Sparse Core Ops, SparseCore 0:
  25.0 52.8 all-reduce.12
  79.7 30.7 all-gather.10
  112.4 30.1 all-gather.8
  144.3 30.1 all-gather.4
  176.2 30.1 all-gather.6
  221.3 72.3 all-reduce.10
  315.0 132.8 all-reduce.14
  474.4 55.8 reduce-scatter.4
  534.3 56.8 reduce-scatter.2
where the time goes:
time: 607 us; the launch traced here: 598 us
  waiting for transfers between devices  326 us (54%)
  blocking collectives  110 us (18%)
  matrix products  66.2 us (11%)
  local copies, waits for them, and re-layouts  39.9 us (7%)
  other arithmetic  38.5 us (6%)
  between operations  16.2 us (3%)
    psum x2, waiting for transfers between devices, network(): mixed = lax.psum(partial_out, 'col').astype(jnp.float32)  186 us
    reduce_scatter x2, waiting for transfers between devices, reduce_gradient(): lax.psum_scatter(contract_first(left, right), ('dp', 'row'), scatter_dime...  104 us
    all_gather x1, blocking collectives, body(): lax.all_gather(teacher_sums, 'col', axis=3, tiled=True)  62.1 us
    all_gather x1, blocking collectives, body(): lax.all_gather(student_sums, 'col', axis=3, tiled=True)  38.8 us
    unnamed x10, waiting for transfers between devices  36.1 us
    dot_general x6, matrix products, contract_last(): lax.dot_general(left, right, (((1,), (1,)), ((), ())), preferred_element_...  29 us
    unnamed x77, local copies, waits for them, and re-layouts  21.6 us
    dot_general x2, matrix products, contract_first(): lax.dot_general(left, right, (((0,), (0,)), ((), ())), preferred_element_...  17.3 us
  transfers between devices with their start and end apart: 9, of which 5 were waited for; matrix products, arithmetic and copies ran while one was open for 15% of the time, Pallas kernels for 0%

commit v1 on v0

--- a/solution.py
+++ b/solution.py
@@ -3,6 +3,7 @@
 import jax.numpy as jnp
 from jax import lax
 from jax.sharding import PartitionSpec as P
+from jax.lax import all_gather
 
 D = 1152
 CLASSES = 1000
@@ -92,6 +93,12 @@
 
 
 def network(state, mods, patch_weight, out_weight, pos, up_product, down_product):
+
+    def _detail_words(xin):
+        out_arr = all_gather(xin, "col")
+        view_out = jnp.sum(out_arr, 0)
+        return view_out
+
     samples = state.shape[0]
     tokens = state.reshape(samples * SEQ, PATCH).astype(jnp.bfloat16)
     base = (
@@ -106,7 +113,7 @@
     pre = up_product(act)
     hidden = jax.nn.gelu(pre, approximate=True).astype(jnp.bfloat16)
     partial_out = down_product(hidden).astype(jnp.bfloat16)
-    mixed = lax.psum(partial_out, "col").astype(jnp.float32)
+    mixed = _detail_words(partial_out).astype(jnp.float32)
     later = base + gate * mixed.reshape(samples, SEQ, D)
     final, reciprocal = layer_norm(later)
     velocity = contract_last(final.astype(jnp.bfloat16).reshape(samples * SEQ, D), out_weight)

time: 607 us -> 746 us (1.23)
  waiting for transfers between devices: 326 us -> 451 us
  other arithmetic: 38.5 us -> 55.4 us
    all_gather x0 -> x3, waiting for transfers between devices: none -> 304 us  [_detail_words(): out_arr = all_gather(xin, 'col')]
    psum x2 -> x0, waiting for transfers between devices: 186 us -> none  [network(): mixed = lax.psum(partial_out, 'col').astype(jnp.float32)]
    reduce_sum x0 -> x3, other arithmetic: none -> 17.3 us  [_detail_words(): view_out = jnp.sum(out_arr, 0)]
    unnamed x10 -> x11, waiting for transfers between devices: 36.1 us -> 42.9 us
    unnamed x77 -> x71, local copies, waits for them, and re-layouts: 21.6 us -> 19.6 us
  transfers between devices with their start and end apart: 9 -> 10, of which waited for: 5 -> 6; matrix products, arithmetic and copies ran while one was open for 15% -> 17% of each run, Pallas kernels for 0% -> 0%
where the time goes in v1:
time: 746 us; the launch traced here: 739 us
  waiting for transfers between devices  451 us (60%)
  blocking collectives  110 us (15%)
  matrix products  67.6 us (9%)
  other arithmetic  55.4 us (7%)
  local copies, waits for them, and re-layouts  38.1 us (5%)
  between operations  16.5 us (2%)
    all_gather x3, waiting for transfers between devices, _detail_words(): out_arr = all_gather(xin, 'col')  304 us
    reduce_scatter x2, waiting for transfers between devices, reduce_gradient(): lax.psum_scatter(contract_first(left, right), ('dp', 'row'), scatter_dime...  103 us
    all_gather x1, blocking collectives, body(): lax.all_gather(teacher_sums, 'col', axis=3, tiled=True)  62.6 us
    unnamed x11, waiting for transfers between devices  42.9 us
    all_gather x1, blocking collectives, body(): lax.all_gather(student_sums, 'col', axis=3, tiled=True)  38.2 us
    dot_general x6, matrix products, contract_last(): lax.dot_general(left, right, (((1,), (1,)), ((), ())), preferred_element_...  28.8 us
    unnamed x71, local copies, waits for them, and re-layouts  19.6 us
    dot_general x2, matrix products, contract_first(): lax.dot_general(left, right, (((0,), (0,)), ((), ())), preferred_element_...  17.6 us
  transfers between devices with their start and end apart: 10, of which 6 were waited for; matrix products, arithmetic and copies ran while one was open for 17% of the time, Pallas kernels for 0%

profile of v1, /device:TPU:0, one launch (start us, length us, event | category | flops | bytes accessed | tf_op | source)
XLA Modules:
  0.0 739.3 jit_solution(6603615169965612273)
XLA Ops:
  11.1 9.5 %all-reduce.4 = (s32[24]{0:T(128)S(1)}, s32[24]{0:T(128)S(1)}) all-reduce(s32[24]{0:T(128)S(1)} %dynamic-update-slice, s32[24]{0:T(128)S(1)} %dynamic-update-slice.1), channel_id=1, replica_groups=mesh['dp'=2,'row'=4,'col'=4] {'dp','row'}, use_global_device_ids=true, to_apply=%add | all-reduce | flops 48 | bytes 384
  37.4 40.4 %all-reduce.8.cloned.1.call-done = (f32[24,1,3,288]{3,1,2,0:T(1,128)}, f32[24,2,3,288]{3,1,2,0:T(2,128)}) async-done(((f32[24,1,3,288]{3,1,2,0:T(1,128)}, f32[24,2,3,288]{3,1,2,0:T(2,128)}), (f32[24,1,3,288]{3,1,2,0:T(1,128)}, f32[24,2,3,288]{3,1,2,0:T(2,128)})) %all-reduce.8.cloned.1.call-update) | async-done | bytes 248848
  81.1 62.6 %all_gather.49 = f32[3,2,3,1152]{2,1,0,3:T(2,128)S(1)} all-gather(f32[3,2,3,288]{2,1,0,3:T(2,128)} %copy.57), channel_id=1, replica_groups=mesh['dp'=2,'row'=4,'col'=4] {'col'}, dimensions={3}, use_global_device_ids=true | all-gather | bytes 103680 | tf_op jit(solution)/shard_map/all_gather | solution.py:177
  143.8 3.9 fusion.98
  147.7 4.6 copy.81
  156.3 9.5 %convolution_convert_fusion.1 = bf16[768,1152]{1,0:T(8,128)(2,1)} fusion(bf16[1152,1152]{1,0:T(8,128)(2,1)} %all-gather.17.cloned.1.call-done, bf16[768,1152]{1,0:T(8,128)(2,1)} %bitcast.129, bf16[1152,1152]{1,0:T(8,128)(2,1)} %all-gather.15.cloned.1.call-done), kind=kOutput, calls=%fused_computation.59 | convolution fusion | flops 4085710848 | bytes 8847360 | tf_op jit(solution)/shard_map/dot_general | solution.py:84
  174.5 38.2 %all_gather.44 = f32[3,1,3,1152]{2,1,0,3:T(1,128)} all-gather(f32[3,1,3,288]{2,1,0,3:T(1,128)} %copy.52), channel_id=1, replica_groups=mesh['dp'=2,'row'=4,'col'=4] {'col'}, dimensions={3}, use_global_device_ids=true | all-gather | bytes 51840 | tf_op jit(solution)/shard_map/all_gather | solution.py:178
  212.8 4.6 copy.53
  219.0 4.7 add_convert_fusion.2
  223.7 6.7 fusion.110
  230.4 7.3 convolution_convert_fusion.2
  238.0 4.6 copy.82
  244.8 91.1 %all-gather.21.cloned.1.call-done = bf16[3072,1152]{1,0:T(8,128)(2,1)} async-done(((bf16[768,1152]{1,0:T(8,128)(2,1)}), bf16[3072,1152]{1,0:T(8,128)(2,1)}) %all-gather.21.cloned.1.call-update) | async-done | bytes 7077904 | tf_op jit(solution)/shard_map/all_gather | solution.py:98
  335.9 5.8 reduce_sum.169
  353.4 9.5 %convolution_convert_fusion = bf16[768,1152]{1,0:T(8,128)(2,1)} fusion(bf16[1152,1152]{1,0:T(8,128)(2,1)} %all-gather.17.cloned.1.call-done, bf16[768,1152]{1,0:T(8,128)(2,1)} %bitcast.130, bf16[1152,1152]{1,0:T(8,128)(2,1)} %all-gather.15.cloned.1.call-done), kind=kOutput, calls=%fused_computation.58 | convolution fusion | flops 4085710848 | bytes 8847360 | tf_op jit(solution)/shard_map/dot_general | solution.py:84
  363.9 100.0 %all-gather.19.cloned.1.call-done = bf16[3072,1152]{1,0:T(8,128)(2,1)} async-done(((bf16[768,1152]{1,0:T(8,128)(2,1)}), bf16[3072,1152]{1,0:T(8,128)(2,1)}) %all-gather.19.cloned.1.call-update) | async-done | bytes 7077904 | tf_op jit(solution)/shard_map/all_gather | solution.py:98
  463.9 5.8 reduce_sum.164
  478.7 113.2 %all-gather.23.cloned.1.call-done = bf16[3072,1152]{1,0:T(8,128)(2,1)} async-done(((bf16[768,1152]{1,0:T(8,128)(2,1)}), bf16[3072,1152]{1,0:T(8,128)(2,1)}) %all-gather.23.cloned.1.call-update) | async-done | bytes 7077904 | tf_op jit(solution)/shard_map/all_gather | solution.py:98
  591.8 5.8 reduce_sum.174
  603.3 4.6 fusion.93
  610.9 5.1 fusion.90
  616.1 12.5 %fusion.114 = f32[1152,1152]{1,0:T(8,128)} fusion(bf16[768,1152]{1,0:T(8,128)(2,1)} %bitcast.126, f32[768,1152]{1,0:T(8,128)} %fusion.110, bf16[768,1152]{1,0:T(8,128)(2,1)} %bitcast.128, bf16[1152,1152]{1,0:T(8,128)(2,1)} %all-gather.13.cloned.1.call-done), kind=kOutput, calls=%fused_computation.205 | convolution fusion | flops 4093673472 | bytes 15040512 | tf_op jit(solution)/shard_map/dot_general | solution.py:90
  628.6 42.6 %reduce-scatter.5.cloned.1.call-done = f32[144,1152]{1,0:T(8,128)} async-done(((f32[1152,1152]{1,0:T(8,128)}), f32[144,1152]{1,0:T(8,128)}) %reduce-scatter.5.cloned.1.call-update) | async-done | bytes 663568 | tf_op jit(solution)/shard_map/reduce_scatter | solution.py:127
  671.2 60.7 %reduce-scatter.3.cloned.1.call-done = f32[144,1152]{1,0:T(8,128)} async-done(((f32[1152,1152]{1,0:T(8,128)}), f32[144,1152]{1,0:T(8,128)}) %reduce-scatter.3.cloned.1.call-update) | async-done | bytes 663568 | tf_op jit(solution)/shard_map/reduce_scatter | solution.py:127
  (159 shorter events, 69.6 us)
Async XLA Ops:
  7.2 14.0 %copy-start = (bf16[1000,1152]{1,0:T(8,128)(2,1)S(1)}, bf16[1000,1152]{1,0:T(8,128)(2,1)}, u32[]{:S(2)}) copy-start(bf16[1000,1152]{1,0:T(8,128)(2,1)} %param.19) | copy-start | bytes 6912004
  7.2 20.4 %copy-start.25 = (s32[3]{0:T(128)S(1)}, s32[3]{0:T(128)}, u32[]{:S(2)}) copy-start(s32[3]{0:T(128)} %param.17) | copy-start | bytes 40
  7.2 16.6 %copy-start.8 = (bf16[144,3,288]{2,0,1:T(8,128)(2,1)S(1)}, bf16[144,3,288]{2,0,1:T(8,128)(2,1)}, u32[]{:S(2)}) copy-start(bf16[144,3,288]{2,0,1:T(8,128)(2,1)} %param.21) | copy-start | bytes 746500
  7.2 21.0 %copy-start.26 = (s32[3]{0:T(128)S(1)}, s32[3]{0:T(128)}, u32[]{:S(2)}) copy-start(s32[3]{0:T(128)} %param.18) | copy-start | bytes 40
  7.2 21.0 %copy-start.18 = (f32[3,32,128]{2,1,0:T(8,128)S(1)}, f32[3,32,128]{2,1,0:T(8,128)}, u32[]{:S(2)}) copy-start(f32[3,32,128]{2,1,0:T(8,128)} %param.15) | copy-start | bytes 147460
  7.2 70.6 %all-reduce.8.cloned.1.call-start = ((), (), s32[]{:S(2)}) async-start(), calls=%async_computation.11 | async-start | bytes 663552
  24.8 131.5 %all-gather.15.cloned.1.call-start = ((), (), s32[]{:S(2)}) async-start(), calls=%async_computation.4 | async-start | bytes 2985984 | tf_op jit(solution)/shard_map/all_gather | solution.py:186
  25.6 130.7 %all-gather.17.cloned.1.call-start = ((), (), s32[]{:S(2)}) async-start(), calls=%async_computation.5 | async-start | bytes 2985984 | tf_op jit(solution)/shard_map/all_gather | solution.py:187
  26.3 197.4 %all-gather.11.cloned.1.call-start = ((), (), s32[]{:S(2)}) async-start(), calls=%async_computation.2 | async-start | bytes 2985984 | tf_op jit(solution)/shard_map/all_gather | solution.py:224
  26.9 203.5 %all-gather.13.cloned.1.call-start = ((), (), s32[]{:S(2)}) async-start(), calls=%async_computation.3 | async-start | bytes 2985984 | tf_op jit(solution)/shard_map/all_gather | solution.py:228
  27.5 308.4 %all-gather.21.cloned.1.call-start = ((), (), s32[]{:S(2)}) async-start(), calls=%async_computation.9 | async-start | bytes 8847360 | tf_op jit(solution)/shard_map/all_gather | solution.py:98
  165.8 298.1 %all-gather.19.cloned.1.call-start = ((), (), s32[]{:S(2)}) async-start(), calls=%async_computation.8 | async-start | bytes 8847360 | tf_op jit(solution)/shard_map/all_gather | solution.py:98
  169.6 3.1 copy-start.19
  174.5 44.4 %copy-start.20 = (f32[3,256]{1,0:T(4,128)S(1)}, f32[3,256]{1,0:T(4,128)}, u32[]{:S(2)}) copy-start(f32[3,256]{1,0:T(4,128)} %copy-done.19) | copy-start | bytes 9220
  174.5 44.4 %copy-start.21 = (f32[3,256]{1,0:T(4,128)S(1)}, f32[3,256]{1,0:T(4,128)}, u32[]{:S(2)}) copy-start(f32[3,256]{1,0:T(4,128)} %add_rsqrt_fusion.5) | copy-start | bytes 9220
  237.7 4.9 copy-start.17
  237.7 354.1 %all-gather.23.cloned.1.call-start = ((), (), s32[]{:S(2)}) async-start(), calls=%async_computation.10 | async-start | bytes 8847360 | tf_op jit(solution)/shard_map/all_gather | solution.py:98
  348.2 2.6 copy-start.16
  363.0 308.3 %reduce-scatter.5.cloned.1.call-start = ((), (), s32[]{:S(2)}) async-start(), calls=%async_computation.7 | async-start | bytes 5971968 | tf_op jit(solution)/shard_map/reduce_scatter | solution.py:127
  603.3 4.7 copy-start.3
  603.3 4.7 copy-start.11
  608.0 2.9 copy-start.27
  616.0 116.0 %reduce-scatter.3.cloned.1.call-start = ((), (), s32[]{:S(2)}) async-start(), calls=%async_computation.6 | async-start | bytes 5971968 | tf_op jit(solution)/shard_map/reduce_scatter | solution.py:127
  616.1 115.9 %copy-start.1 = (bf16[1000,1152]{1,0:T(8,128)(2,1)S(1)}, bf16[1000,1152]{1,0:T(8,128)(2,1)}, u32[]{:S(2)}) copy-start(bf16[1000,1152]{1,0:T(8,128)(2,1)} %param.19) | copy-start | bytes 6912004
  (14 other events, 24.4 us)
Sparse Core Ops, SparseCore 0:
  25.0 52.7 all-reduce.7
  79.7 30.7 all-gather.14
  112.3 30.1 all-gather.16
  144.2 30.1 all-gather.10
  176.1 30.1 all-gather.12
  207.7 128.1 all-gather.20
  337.5 126.3 all-gather.18
  465.4 126.3 all-gather.22
  616.1 55.0 reduce-scatter.4
  675.1 56.8 reduce-scatter.2
